TPU v7x, 128 devices: a whole 4x4x4 slice. The times are simulated.
128 devices in a mesh: grp: 2 (over core), dev: 64 (over x, z, y).
Axes of the slice: x: 4, y: 4, z: 4, core: 2. Of those that a mesh axis runs over, the one named last changes fastest.
Arguments:
- state: float32 [2, 24, 24, 16384], P(None, None, None, ('grp', 'dev')), may hold values from -6 to 6
- hamiltonian: float32 [24, 24], replicated, may hold values from -1.2 to 1.2
- mode_rates: float32 [96], replicated, may hold values from 0.05 to 2
- ado_modes: int32 [3, 16384], P(None, ('grp', 'dev')), may hold values from 0 to 96
- link_src: int32 [8, 16384], P(None, ('grp', 'dev')), may hold values from 0 to 383, as said below
- link_site: int32 [8, 16384], P(None, ('grp', 'dev')), may hold values from 0 to 23
- link_coef: float32 [4, 8, 16384], P(None, None, ('grp', 'dev')), may hold values from -2.4 to 2.4
- send_ids: int32 [128, 256], P(('grp', 'dev')), may hold values from 0 to 127
- step_units: int32 [], replicated, may hold values from 12 to 16
Outputs:
- new_state: float32 [2, 24, 24, 16384], P(None, None, None, ('grp', 'dev'))
- error_norm: float32 [], replicated
Inputs may be any that keep to these rules, and one draw needn't show every extreme that they name: `link_src`: on each device every received position 128 to 383 is named by 1 to 4 couplings of that device's matrices, and some position by exactly 4.
All inputs are finite; a program needn't handle non-finite values.
Results may differ from a plain program's by a relative error of at most 0.0003.
Values sent between devices are 32-bit elements; how exact they have to be, the bound alone decides.
No kernel may reach another device: no remote copies, remote signals or barrier semaphores. Data moves between devices by JAX's collectives and lax.ppermute only.
A program may use at most 128 MiB of HBM per device.

v0:
```python
import functools
import jax
import jax.numpy as jnp
from jax import lax
from jax.sharding import Mesh
from jax.sharding import PartitionSpec as P

DEV = ("dev_0", "dev_1", "dev_2")
GRP_DEV = ("grp", "dev_0", "dev_1", "dev_2")
TABLEAU = (
    (0.2,),
    (3.0 / 40, 9.0 / 40),
    (44.0 / 45, -56.0 / 15, 32.0 / 9),
    (19372.0 / 6561, -25360.0 / 2187, 64448.0 / 6561, -212.0 / 729),
    (9017.0 / 3168, -355.0 / 33, 46732.0 / 5247, 49.0 / 176, -5103.0 / 18656),
    (35.0 / 384, 0.0, 500.0 / 1113, 125.0 / 192, -2187.0 / 6784, 11.0 / 84),
)
ERRORS = (71.0 / 57600, 0.0, -71.0 / 16695, 71.0 / 1920, -17253.0 / 339200, 22.0 / 525, -1.0 / 40)
ABS_TOL = 0.001
REL_TOL = 0.01
UNIT_STEP = 1.0 / 64
HIGHEST = lax.Precision.HIGHEST


def one_axis_at_a_time(shard, axes):
    return functools.reduce(lax.psum, axes, shard)


def commute(symmetric, current):
    left_prod = jnp.einsum("ab,sbcx->sacx", symmetric, current, precision=HIGHEST)
    right_prod = jnp.einsum("sabx,bc->sacx", current, symmetric, precision=HIGHEST)
    return left_prod - right_prod


def decay_rates(ado_modes, mode_rates):
    extended = jnp.concatenate([mode_rates, jnp.zeros((1,), mode_rates.dtype)])
    levels = jnp.arange(extended.shape[0], dtype=jnp.int32)
    hits = (ado_modes[:, None, :] == levels[None, :, None]).astype(mode_rates.dtype)
    return jnp.sum(hits * extended[None, :, None], axis=(0, 1))


def selector(indices, count, dtype):
    levels = jnp.arange(count, dtype=jnp.int32)
    return (levels[:, None] == indices.reshape(-1)[None, :]).astype(dtype)


def masked_term(source, sites, coef):
    levels = jnp.arange(source.shape[1], dtype=jnp.int32)
    indicator = (levels[:, None] == sites[None, :]).astype(source.dtype)
    row_mask = indicator[:, None, :]
    column_mask = indicator[None, :, :]
    weight_real = coef[0] * row_mask - coef[2] * column_mask
    weight_imag = coef[1] * row_mask - coef[3] * column_mask
    real_part = weight_real * source[0] - weight_imag * source[1]
    imag_part = weight_real * source[1] + weight_imag * source[0]
    return jnp.stack([imag_part, -real_part])


def shards(
    state, hamiltonian, mode_rates, ado_modes, link_src, link_site, link_coef, send_ids, step_units
):
    outgoing = send_ids[0]
    symmetric = 0.5 * (hamiltonian + hamiltonian.T)
    decay = decay_rates(ado_modes, mode_rates)
    step_size = step_units.astype(state.dtype) * UNIT_STEP
    groups = lax.axis_size("grp")
    members = lax.axis_size(DEV)
    sites = state.shape[1]
    owned = state.shape[3]
    received = outgoing.shape[0]
    links = link_src.shape[0]
    flat_rows = 2 * sites * sites
    pack_table = selector(outgoing, owned, state.dtype)
    link_table = selector(link_src, owned + received, state.dtype)

    def evaluate(current):
        flat_current = current.reshape(flat_rows, owned)
        packed = jnp.dot(flat_current, pack_table, precision=HIGHEST).reshape(
            2, sites, sites, received
        )
        commutator = commute(symmetric, current)
        total = jnp.stack([commutator[1], -commutator[0]]) - decay[None, None, None, :] * current
        moved = lax.all_to_all(packed, GRP_DEV, split_axis=3, concat_axis=3, tiled=True)
        combined = jnp.concatenate([flat_current, moved.reshape(flat_rows, received)], axis=1)
        fetched = jnp.dot(combined, link_table, precision=HIGHEST)
        for link in range(links):
            start = link * owned
            source = fetched[:, start : start + owned].reshape(2, sites, sites, owned)
            total = total + masked_term(source, link_site[link], link_coef[:, link])
        return total

    sections = [evaluate(state)]
    inner = state
    for weights in TABLEAU:
        inner = state
        for weight, section in zip(weights, sections):
            if weight != 0.0:
                inner = inner + step_size * weight * section
        sections.append(evaluate(inner))
    error = jnp.zeros_like(state)
    for weight, section in zip(ERRORS, sections):
        if weight != 0.0:
            error = error + step_size * weight * section
    scale = ABS_TOL + REL_TOL * jnp.maximum(jnp.abs(state), jnp.abs(inner))
    partial_sum = jnp.sum(jnp.square(error / scale))
    total_sum = one_axis_at_a_time(partial_sum, GRP_DEV)
    entries = 2 * sites * sites * owned * groups * members
    return (inner, jnp.sqrt(total_sum / entries))


def solution(mesh):
    finer = Mesh(
        mesh.devices.reshape(mesh.shape["grp"], 4, 4, 4), ("grp", "dev_0", "dev_1", "dev_2")
    )
    return jax.shard_map(
        shards,
        mesh=finer,
        in_specs=(
            P(None, None, None, GRP_DEV),
            P(),
            P(),
            P(None, GRP_DEV),
            P(None, GRP_DEV),
            P(None, GRP_DEV),
            P(None, None, GRP_DEV),
            P(GRP_DEV, None),
            P(),
        ),
        out_specs=(P(None, None, None, GRP_DEV), P()),
        check_vma=False,
    )
```

profile of v0, /device:TPU:0, one launch (start us, length us, event | category | flops | bytes accessed | tf_op | source)
XLA Modules:
  0.0 502.5 jit_solution(1082587879265455247)
XLA Ops:
  8.1 7.2 %reshape.4447 = f32[128,1,2304]{2,1,0:T(1,128)} reshape(f32[256,2,24,24]{3,2,1,0:T(8,128)} %bitcast.336) | data formatting | bytes 2359296
  15.4 11.3 %all-to-all-start = ((f32[128,1,2304]{2,1,0:T(1,128)}), f32[128,1,2304]{2,1,0:T(1,128)S(1)}, u32[]{:S(2)}, u32[]{:S(2)}) async-start(f32[128,1,2304]{2,1,0:T(1,128)} %reshape.4447), calls=%async_computation | async-start | bytes 2359296 | tf_op jit(solution)/shard_map/all_to_all | solution.py:83
  33.1 13.0 %all-to-all-done = f32[128,1,2304]{2,1,0:T(1,128)S(1)} async-done(((f32[128,1,2304]{2,1,0:T(1,128)}), f32[128,1,2304]{2,1,0:T(1,128)S(1)}, u32[]{:S(2)}, u32[]{:S(2)}) %all-to-all-start) | async-done | bytes 1179680 | tf_op jit(solution)/shard_map/all_to_all | solution.py:83
  75.5 7.2 %reshape.4449 = f32[128,1,2304]{2,1,0:T(1,128)} reshape(f32[256,2,24,24]{3,2,1,0:T(8,128)} %bitcast.338) | data formatting | bytes 2359296
  91.3 16.6 %all-to-all-done.1 = f32[128,1,2304]{2,1,0:T(1,128)} async-done(((f32[128,1,2304]{2,1,0:T(1,128)}), f32[128,1,2304]{2,1,0:T(1,128)}, u32[]{:S(2)}, u32[]{:S(2)}) %all-to-all-start.1) | async-done | bytes 1179680 | tf_op jit(solution)/shard_map/all_to_all | solution.py:83
  138.8 7.2 %reshape.4451 = f32[128,1,2304]{2,1,0:T(1,128)} reshape(f32[256,2,24,24]{3,2,1,0:T(8,128)} %bitcast.340) | data formatting | bytes 2359296
  154.5 16.6 %all-to-all-done.2 = f32[128,1,2304]{2,1,0:T(1,128)} async-done(((f32[128,1,2304]{2,1,0:T(1,128)}), f32[128,1,2304]{2,1,0:T(1,128)}, u32[]{:S(2)}, u32[]{:S(2)}) %all-to-all-start.2) | async-done | bytes 1179680 | tf_op jit(solution)/shard_map/all_to_all | solution.py:83
  201.4 7.2 %reshape.4453 = f32[128,1,2304]{2,1,0:T(1,128)} reshape(f32[256,2,24,24]{3,2,1,0:T(8,128)} %bitcast.342) | data formatting | bytes 2359296
  218.1 15.8 %all-to-all-done.3 = f32[128,1,2304]{2,1,0:T(1,128)} async-done(((f32[128,1,2304]{2,1,0:T(1,128)}), f32[128,1,2304]{2,1,0:T(1,128)}, u32[]{:S(2)}, u32[]{:S(2)}) %all-to-all-start.3) | async-done | bytes 1179680 | tf_op jit(solution)/shard_map/all_to_all | solution.py:83
  261.7 6.3 %copy.1048 = f32[2,24,24,256]{2,1,0,3:T(8,128)} copy(f32[2,24,24,256]{3,1,2,0:T(8,128)} %fusion.278) | data formatting | bytes 2359296 | tf_op jit(solution)/shard_map/dot_general | solution.py:78
  268.1 7.2 %reshape.4455 = f32[128,1,2304]{2,1,0:T(1,128)} reshape(f32[256,2,24,24]{3,2,1,0:T(8,128)} %bitcast.344) | data formatting | bytes 2359296
  283.8 16.6 %all-to-all-done.4 = f32[128,1,2304]{2,1,0:T(1,128)} async-done(((f32[128,1,2304]{2,1,0:T(1,128)}), f32[128,1,2304]{2,1,0:T(1,128)}, u32[]{:S(2)}, u32[]{:S(2)}) %all-to-all-start.4) | async-done | bytes 1179680 | tf_op jit(solution)/shard_map/all_to_all | solution.py:83
  306.2 6.7 %reshape.4456 = f32[256,2,24,24]{3,2,1,0:T(8,128)} reshape(f32[128,2304]{1,0:T(8,128)} %reduce.4) | data formatting | bytes 2359296
  330.9 6.3 %copy.1088 = f32[2,24,24,256]{2,1,0,3:T(8,128)} copy(f32[2,24,24,256]{3,1,2,0:T(8,128)} %fusion.276) | data formatting | bytes 2359296 | tf_op jit(solution)/shard_map/dot_general | solution.py:78
  337.3 7.2 %reshape.4457 = f32[128,1,2304]{2,1,0:T(1,128)} reshape(f32[256,2,24,24]{3,2,1,0:T(8,128)} %bitcast.346) | data formatting | bytes 2359296
  353.9 15.8 %all-to-all-done.5 = f32[128,1,2304]{2,1,0:T(1,128)} async-done(((f32[128,1,2304]{2,1,0:T(1,128)}), f32[128,1,2304]{2,1,0:T(1,128)}, u32[]{:S(2)}, u32[]{:S(2)}) %all-to-all-start.5) | async-done | bytes 1179680 | tf_op jit(solution)/shard_map/all_to_all | solution.py:83
  375.5 6.7 %reshape.4458 = f32[256,2,24,24]{3,2,1,0:T(8,128)} reshape(f32[128,2304]{1,0:T(8,128)} %reduce.5) | data formatting | bytes 2359296
  382.2 6.5 %copy.1089 = f32[2,24,24,256]{3,2,1,0:T(8,128)} copy(f32[2,24,24,256]{2,1,0,3:T(8,128)} %bitcast.347) | data formatting | bytes 2359296 | tf_op jit(solution)/shard_map/all_to_all | solution.py:83
  406.7 7.2 %reshape.4459 = f32[128,1,2304]{2,1,0:T(1,128)} reshape(f32[256,2,24,24]{3,2,1,0:T(8,128)} %bitcast.348) | data formatting | bytes 2359296
  422.4 16.6 %all-to-all-done.6 = f32[128,1,2304]{2,1,0:T(1,128)} async-done(((f32[128,1,2304]{2,1,0:T(1,128)}), f32[128,1,2304]{2,1,0:T(1,128)}, u32[]{:S(2)}, u32[]{:S(2)}) %all-to-all-start.6) | async-done | bytes 1179680 | tf_op jit(solution)/shard_map/all_to_all | solution.py:83
  444.8 6.7 %reshape.4460 = f32[256,2,24,24]{3,2,1,0:T(8,128)} reshape(f32[128,2304]{1,0:T(8,128)} %reduce.6) | data formatting | bytes 2359296
  470.9 9.9 %psum.29 = f32[]{:T(128)} all-reduce(f32[]{:T(128)} %psum.28), channel_id=1, replica_groups=mesh['grp'=2,'dev_0'=4,'dev_1'=4,'dev_2'=4] {'dev_0'}, use_global_device_ids=true, to_apply=%region_3.0 | all-reduce | flops 1 | bytes 8 | tf_op jit(solution)/shard_map/psum | solution.py:26
  480.8 9.7 %psum.30 = f32[]{:T(128)} all-reduce(f32[]{:T(128)} %psum.29), channel_id=1, replica_groups=mesh['grp'=2,'dev_0'=4,'dev_1'=4,'dev_2'=4] {'dev_1'}, use_global_device_ids=true, to_apply=%region_4.0 | all-reduce | flops 1 | bytes 8 | tf_op jit(solution)/shard_map/psum | solution.py:26
  490.5 10.0 %psum.31 = f32[]{:T(128)} all-reduce(f32[]{:T(128)} %psum.30), channel_id=1, replica_groups=mesh['grp'=2,'dev_0'=4,'dev_1'=4,'dev_2'=4] {'dev_2'}, use_global_device_ids=true, to_apply=%region_5.0 | all-reduce | flops 1 | bytes 8 | tf_op jit(solution)/shard_map/psum | solution.py:26
  (687 shorter events, 254.4 us)
Async XLA Ops:
  15.4 11.4 %copy-start.263 = (f32[4,8,128]{2,1,0:T(8,128)S(1)}, f32[4,8,128]{2,1,0:T(8,128)}, u32[]{:S(2)}) copy-start(f32[4,8,128]{2,1,0:T(8,128)} %param.15) | copy-start | bytes 49156
  15.4 12.1 %copy-start.264 = (s32[8,128]{1,0:T(8,128)S(1)}, s32[8,128]{1,0:T(8,128)}, u32[]{:S(2)}) copy-start(s32[8,128]{1,0:T(8,128)} %param.14) | copy-start | bytes 12292
  15.4 12.1 %copy-start.255 = (f32[24,24]{1,0:T(8,128)S(1)}, f32[24,24]{1,0:T(8,128)}, u32[]{:S(2)}) copy-start(f32[24,24]{1,0:T(8,128)} %param.10) | copy-start | bytes 6916
  15.4 12.2 %copy-start.266 = (f32[96]{0:T(128)S(1)}, f32[96]{0:T(128)}, u32[]{:S(2)}) copy-start(f32[96]{0:T(128)} %param.11) | copy-start | bytes 1156
  15.4 12.3 %copy-start.265 = (s32[3,128]{1,0:T(4,128)S(1)}, s32[3,128]{1,0:T(4,128)}, u32[]{:S(2)}) copy-start(s32[3,128]{1,0:T(4,128)} %param.12) | copy-start | bytes 4612
  15.4 15.5 %copy-start = (f32[2,24,24,128]{3,2,1,0:T(8,128)S(1)}, f32[2,24,24,128]{3,2,1,0:T(8,128)}, u32[]{:S(2)}) copy-start(f32[2,24,24,128]{3,2,1,0:T(8,128)} %param.9) | copy-start | bytes 1769476
  15.4 30.7 %all-to-all-start = ((f32[128,1,2304]{2,1,0:T(1,128)}), f32[128,1,2304]{2,1,0:T(1,128)S(1)}, u32[]{:S(2)}, u32[]{:S(2)}) async-start(f32[128,1,2304]{2,1,0:T(1,128)} %reshape.4447), calls=%async_computation | async-start | bytes 2359296 | tf_op jit(solution)/shard_map/all_to_all | solution.py:83
  56.4 5.3 %copy-start.248 = (s32[8,128]{1,0:T(8,128)S(1)}, s32[8,128]{1,0:T(8,128)}, u32[]{:S(2)}) copy-start(s32[8,128]{1,0:T(8,128)} %param.13) | copy-start | bytes 12292
  82.7 25.2 %all-to-all-start.1 = ((f32[128,1,2304]{2,1,0:T(1,128)}), f32[128,1,2304]{2,1,0:T(1,128)}, u32[]{:S(2)}, u32[]{:S(2)}) async-start(f32[128,1,2304]{2,1,0:T(1,128)} %reshape.4449), calls=%async_computation.1 | async-start | bytes 2359296 | tf_op jit(solution)/shard_map/all_to_all | solution.py:83
  146.0 25.1 %all-to-all-start.2 = ((f32[128,1,2304]{2,1,0:T(1,128)}), f32[128,1,2304]{2,1,0:T(1,128)}, u32[]{:S(2)}, u32[]{:S(2)}) async-start(f32[128,1,2304]{2,1,0:T(1,128)} %reshape.4451), calls=%async_computation.2 | async-start | bytes 2359296 | tf_op jit(solution)/shard_map/all_to_all | solution.py:83
  208.7 25.2 %all-to-all-start.3 = ((f32[128,1,2304]{2,1,0:T(1,128)}), f32[128,1,2304]{2,1,0:T(1,128)}, u32[]{:S(2)}, u32[]{:S(2)}) async-start(f32[128,1,2304]{2,1,0:T(1,128)} %reshape.4453), calls=%async_computation.3 | async-start | bytes 2359296 | tf_op jit(solution)/shard_map/all_to_all | solution.py:83
  275.3 25.1 %all-to-all-start.4 = ((f32[128,1,2304]{2,1,0:T(1,128)}), f32[128,1,2304]{2,1,0:T(1,128)}, u32[]{:S(2)}, u32[]{:S(2)}) async-start(f32[128,1,2304]{2,1,0:T(1,128)} %reshape.4455), calls=%async_computation.4 | async-start | bytes 2359296 | tf_op jit(solution)/shard_map/all_to_all | solution.py:83
  326.3 1.3 copy-start.12
  326.3 1.4 copy-start.13
  326.3 1.4 copy-start.260
  327.7 1.5 copy-start.253
  344.5 25.2 %all-to-all-start.5 = ((f32[128,1,2304]{2,1,0:T(1,128)}), f32[128,1,2304]{2,1,0:T(1,128)}, u32[]{:S(2)}, u32[]{:S(2)}) async-start(f32[128,1,2304]{2,1,0:T(1,128)} %reshape.4457), calls=%async_computation.5 | async-start | bytes 2359296 | tf_op jit(solution)/shard_map/all_to_all | solution.py:83
  382.2 6.5 %copy-start.9 = (f32[2,24,24,128]{3,2,1,0:T(8,128)S(1)}, f32[2,24,24,128]{3,2,1,0:T(8,128)}, u32[]{:S(2)}) copy-start(f32[2,24,24,128]{3,2,1,0:T(8,128)} %copy.1084) | copy-start | bytes 1769476
  397.2 1.5 copy-start.254
  413.9 25.1 %all-to-all-start.6 = ((f32[128,1,2304]{2,1,0:T(1,128)}), f32[128,1,2304]{2,1,0:T(1,128)}, u32[]{:S(2)}, u32[]{:S(2)}) async-start(f32[128,1,2304]{2,1,0:T(1,128)} %reshape.4459), calls=%async_computation.6 | async-start | bytes 2359296 | tf_op jit(solution)/shard_map/all_to_all | solution.py:83
  420.2 37.6 %copy-start.7 = (f32[2,24,24,128]{3,2,1,0:T(8,128)}, f32[2,24,24,128]{3,2,1,0:T(8,128)S(1)}, u32[]{:S(2)}) copy-start(f32[2,24,24,128]{3,2,1,0:T(8,128)S(1)} %copy.1162) | copy-start | bytes 1769476
  465.0 1.3 copy-start.10
  465.0 1.4 copy-start.11
  465.0 1.4 copy-start.262
  (250 other events, 196.8 us)
where the time goes:
time: 509 us; the launch traced here: 503 us
  local copies, waits for them, and re-layouts  194 us (38%)
  waiting for transfers between devices  111 us (22%)
  other arithmetic  59.6 us (12%)
  matrix products  50.3 us (10%)
  starting transfers between devices  48.3 us (9%)
  blocking collectives  32.6 us (6%)
  between operations  6.24 us (1%)
    all_to_all x7, waiting for transfers between devices, evaluate(): lax.all_to_all(packed, GRP_DEV, split_axis=3, concat_axis=3, tiled=True)  111 us
    unnamed x550, local copies, waits for them, and re-layouts  107 us
    all_to_all x7, starting transfers between devices, evaluate(): lax.all_to_all(packed, GRP_DEV, split_axis=3, concat_axis=3, tiled=True)  48.3 us
    all_to_all x8, local copies, waits for them, and re-layouts, evaluate(): lax.all_to_all(packed, GRP_DEV, split_axis=3, concat_axis=3, tiled=True)  41 us
    dot_general x7, local copies, waits for them, and re-layouts, evaluate(): jnp.dot(flat_current, pack_table, precision=HIGHEST)  35.6 us
    all_to_all x7, other arithmetic, evaluate(): lax.all_to_all(packed, GRP_DEV, split_axis=3, concat_axis=3, tiled=True)  34.9 us
    psum x4, blocking collectives, one_axis_at_a_time(): return functools.reduce(lax.psum, axes, shard)  32.6 us
    dot_general x7, matrix products, evaluate(): fetched = jnp.dot(combined, link_table, precision=HIGHEST)  32.2 us
  transfers between devices with their start and end apart: 7, of which 7 were waited for; matrix products, arithmetic and copies ran while one was open for 4% of the time, Pallas kernels for 0%

commit v1 on v0

--- a/solution.py
+++ b/solution.py
@@ -80,7 +80,12 @@
         )
         commutator = commute(symmetric, current)
         total = jnp.stack([commutator[1], -commutator[0]]) - decay[None, None, None, :] * current
-        moved = lax.all_to_all(packed, GRP_DEV, split_axis=3, concat_axis=3, tiled=True)
+        moved = jnp.concatenate(
+            jax.lax.all_to_all(
+                jnp.stack(jnp.split(packed, jax.lax.axis_size(GRP_DEV), 3)), GRP_DEV, 0, 0
+            ),
+            3,
+        )
         combined = jnp.concatenate([flat_current, moved.reshape(flat_rows, received)], axis=1)
         fetched = jnp.dot(combined, link_table, precision=HIGHEST)
         for link in range(links):

time: 509 us -> 1860 us (3.65)
  local copies, waits for them, and re-layouts: 194 us -> 1480 us
  other arithmetic: 59.6 us -> 111 us
    unnamed x550 -> x927, local copies, waits for them, and re-layouts: 107 us -> 1030 us
    another operation x0 -> x21, local copies, waits for them, and re-layouts: none -> 393 us  [the longest x14 352 us: evaluate(): jnp.stack(jnp.split(packed, jax.lax.axis_size(GRP_DEV), 3))]
    reshape x1 -> x21, local copies, waits for them, and re-layouts: 5.35 us -> 52.5 us  [the longest x14 45 us: evaluate(): jnp.concatenate(jax.lax.all_to_all(jnp.stack(jnp.split(packed, jax.lax.ax...]
    add x56, other arithmetic: 7.37 us -> 49.8 us  [masked_term(): imag_part = weight_real * source[1] + weight_imag * source[0]]
    all_to_all x8 -> x1, local copies, waits for them, and re-layouts: 41 us -> 0.51 us  [evaluate(): jax.lax.all_to_all(jnp.stack(jnp.split(packed, jax.lax.axis_size(GRP_DEV)...]
    dot_general x7 -> x1, local copies, waits for them, and re-layouts: 35.6 us -> 0.36 us  [evaluate(): jnp.dot(flat_current, pack_table, precision=HIGHEST)]
  transfers between devices with their start and end apart: 7 -> 7, of which waited for: 7 -> 7; matrix products, arithmetic and copies ran while one was open for 4% -> 1% of each run, Pallas kernels for 0% -> 0%
where the time goes in v1:
time: 1860 us; the launch traced here: 1840 us
  local copies, waits for them, and re-layouts  1480 us (80%)
  other arithmetic  111 us (6%)
  waiting for transfers between devices  106 us (6%)
  matrix products  55.2 us (3%)
  starting transfers between devices  47.4 us (3%)
  blocking collectives  32.6 us (2%)
    unnamed x927, local copies, waits for them, and re-layouts  1030 us
    another operation x14, local copies, waits for them, and re-layouts, evaluate(): jnp.stack(jnp.split(packed, jax.lax.axis_size(GRP_DEV), 3))  352 us
    all_to_all x7, waiting for transfers between devices, evaluate(): jax.lax.all_to_all(jnp.stack(jnp.split(packed, jax.lax.axis_size(GRP_DEV)...  106 us
    add x56, other arithmetic, masked_term(): imag_part = weight_real * source[1] + weight_imag * source[0]  49.8 us
    all_to_all x7, starting transfers between devices, evaluate(): jax.lax.all_to_all(jnp.stack(jnp.split(packed, jax.lax.axis_size(GRP_DEV)...  47.4 us
    reshape x14, local copies, waits for them, and re-layouts, evaluate(): jnp.concatenate(jax.lax.all_to_all(jnp.stack(jnp.split(packed, jax.lax.ax...  45 us
    another operation x7, local copies, waits for them, and re-layouts, evaluate(): moved.reshape(flat_rows, received)  41.3 us
  transfers between devices with their start and end apart: 7, of which 7 were waited for; matrix products, arithmetic and copies ran while one was open for 1% of the time, Pallas kernels for 0%

profile of v1, /device:TPU:0, one launch (start us, length us, event | category | flops | bytes accessed | tf_op | source)
XLA Modules:
  0.0 1835.9 jit_solution(9199271345323218784)
XLA Ops:
  136.8 49.2 %copy.1804 = f32[128,2,24,24,2]{3,2,4,1,0:T(8,128)} copy(f32[128,2,24,24,2]{4,3,2,1,0:T(8,128)} %constant_dynamic-update-slice_fusion) | data formatting | bytes 2359296 | tf_op jit(solution)/shard_map/stack | solution.py:85
  186.0 7.2 reshape.4447
  193.2 11.6 all-to-all-start
  212.3 11.9 all-to-all-done
  396.0 49.2 %copy.1847 = f32[128,2,24,24,2]{3,2,4,1,0:T(8,128)} copy(f32[128,2,24,24,2]{4,3,2,1,0:T(8,128)} %constant_dynamic-update-slice_fusion.128) | data formatting | bytes 2359296 | tf_op jit(solution)/shard_map/stack | solution.py:85
  445.2 7.2 reshape.4449
  461.7 15.6 all-to-all-done.1
  650.9 49.2 %copy.1887 = f32[128,2,24,24,2]{3,2,4,1,0:T(8,128)} copy(f32[128,2,24,24,2]{4,3,2,1,0:T(8,128)} %constant_dynamic-update-slice_fusion.256) | data formatting | bytes 2359296 | tf_op jit(solution)/shard_map/stack | solution.py:85
  700.1 7.2 reshape.4451
  716.8 15.6 all-to-all-done.2
  904.9 49.2 %copy.1928 = f32[128,2,24,24,2]{3,2,4,1,0:T(8,128)} copy(f32[128,2,24,24,2]{4,3,2,1,0:T(8,128)} %constant_dynamic-update-slice_fusion.384) | data formatting | bytes 2359296 | tf_op jit(solution)/shard_map/stack | solution.py:85
  954.1 7.2 reshape.4453
  970.8 15.5 all-to-all-done.3
  1162.7 49.2 %copy.1969 = f32[128,2,24,24,2]{3,2,4,1,0:T(8,128)} copy(f32[128,2,24,24,2]{4,3,2,1,0:T(8,128)} %constant_dynamic-update-slice_fusion.512) | data formatting | bytes 2359296 | tf_op jit(solution)/shard_map/stack | solution.py:85
  1211.9 7.2 reshape.4455
  1228.6 15.5 all-to-all-done.4
  1420.7 49.2 %copy.2010 = f32[128,2,24,24,2]{3,2,4,1,0:T(8,128)} copy(f32[128,2,24,24,2]{4,3,2,1,0:T(8,128)} %constant_dynamic-update-slice_fusion.640) | data formatting | bytes 2359296 | tf_op jit(solution)/shard_map/stack | solution.py:85
  1469.8 7.2 reshape.4457
  1486.5 15.6 all-to-all-done.5
  1678.7 49.2 %copy.2050 = f32[128,2,24,24,2]{3,2,4,1,0:T(8,128)} copy(f32[128,2,24,24,2]{4,3,2,1,0:T(8,128)} %constant_dynamic-update-slice_fusion.768) | data formatting | bytes 2359296 | tf_op jit(solution)/shard_map/stack | solution.py:85
  1743.6 16.5 all-to-all-done.6
  1804.1 9.8 psum.29
  1813.9 9.8 psum.30
  1823.8 9.9 psum.31
  (1092 shorter events, 1296.0 us)
Async XLA Ops:
  84.2 120.6 %copy-start = (f32[2,24,24,128]{3,2,1,0:T(8,128)S(1)}, f32[2,24,24,128]{3,2,1,0:T(8,128)}, u32[]{:S(2)}) copy-start(f32[2,24,24,128]{3,2,1,0:T(8,128)} %param.9) | copy-start | bytes 1769476
  85.3 120.6 %copy-start.7 = (f32[4,8,128]{2,1,0:T(8,128)S(1)}, f32[4,8,128]{2,1,0:T(8,128)}, u32[]{:S(2)}) copy-start(f32[4,8,128]{2,1,0:T(8,128)} %param.15) | copy-start | bytes 49156
  85.3 121.3 %copy-start.8 = (s32[8,128]{1,0:T(8,128)S(1)}, s32[8,128]{1,0:T(8,128)}, u32[]{:S(2)}) copy-start(s32[8,128]{1,0:T(8,128)} %param.14) | copy-start | bytes 12292
  85.3 121.3 %copy-start.6 = (f32[24,24]{1,0:T(8,128)S(1)}, f32[24,24]{1,0:T(8,128)}, u32[]{:S(2)}) copy-start(f32[24,24]{1,0:T(8,128)} %param.10) | copy-start | bytes 6916
  85.3 121.4 %copy-start.10 = (f32[96]{0:T(128)S(1)}, f32[96]{0:T(128)}, u32[]{:S(2)}) copy-start(f32[96]{0:T(128)} %param.11) | copy-start | bytes 1156
  85.3 121.5 %copy-start.9 = (s32[3,128]{1,0:T(4,128)S(1)}, s32[3,128]{1,0:T(4,128)}, u32[]{:S(2)}) copy-start(s32[3,128]{1,0:T(4,128)} %param.12) | copy-start | bytes 4612
  127.3 118.8 %copy-start.5 = (s32[8,128]{1,0:T(8,128)S(1)}, s32[8,128]{1,0:T(8,128)}, u32[]{:S(2)}) copy-start(s32[8,128]{1,0:T(8,128)} %param.13) | copy-start | bytes 12292
  193.2 30.9 %all-to-all-start = ((f32[128,1,2304]{2,1,0:T(1,128)}), f32[128,1,2304]{2,1,0:T(1,128)S(1)}, u32[]{:S(2)}, u32[]{:S(2)}) async-start(f32[128,1,2304]{2,1,0:T(1,128)} %reshape.4447), calls=%async_computation | async-start | bytes 2359296 | tf_op jit(solution)/shard_map/all_to_all | solution.py:84
  452.4 25.0 %all-to-all-start.1 = ((f32[128,1,2304]{2,1,0:T(1,128)}), f32[128,1,2304]{2,1,0:T(1,128)}, u32[]{:S(2)}, u32[]{:S(2)}) async-start(f32[128,1,2304]{2,1,0:T(1,128)} %reshape.4449), calls=%async_computation.1 | async-start | bytes 2359296 | tf_op jit(solution)/shard_map/all_to_all | solution.py:84
  650.9 116.8 %copy-start.2 = (f32[2,24,24,128]{3,1,2,0:T(8,128)S(1)}, f32[2,24,24,128]{3,1,2,0:T(8,128)}, u32[]{:S(2)}) copy-start(f32[2,24,24,128]{3,1,2,0:T(8,128)} %get-tuple-element.21) | copy-start | bytes 1769476
  707.4 25.0 %all-to-all-start.2 = ((f32[128,1,2304]{2,1,0:T(1,128)}), f32[128,1,2304]{2,1,0:T(1,128)}, u32[]{:S(2)}, u32[]{:S(2)}) async-start(f32[128,1,2304]{2,1,0:T(1,128)} %reshape.4451), calls=%async_computation.2 | async-start | bytes 2359296 | tf_op jit(solution)/shard_map/all_to_all | solution.py:84
  904.9 119.8 %copy-start.3 = (f32[2,24,24,128]{3,1,2,0:T(8,128)S(1)}, f32[2,24,24,128]{3,1,2,0:T(8,128)}, u32[]{:S(2)}) copy-start(f32[2,24,24,128]{3,1,2,0:T(8,128)} %get-tuple-element.21) | copy-start | bytes 1769476
  961.3 25.0 %all-to-all-start.3 = ((f32[128,1,2304]{2,1,0:T(1,128)}), f32[128,1,2304]{2,1,0:T(1,128)}, u32[]{:S(2)}, u32[]{:S(2)}) async-start(f32[128,1,2304]{2,1,0:T(1,128)} %reshape.4453), calls=%async_computation.3 | async-start | bytes 2359296 | tf_op jit(solution)/shard_map/all_to_all | solution.py:84
  1162.7 119.5 %copy-start.1 = (f32[2,24,24,128]{3,1,2,0:T(8,128)S(1)}, f32[2,24,24,128]{3,1,2,0:T(8,128)}, u32[]{:S(2)}) copy-start(f32[2,24,24,128]{3,1,2,0:T(8,128)} %get-tuple-element.17) | copy-start | bytes 1769476
  1219.1 25.0 %all-to-all-start.4 = ((f32[128,1,2304]{2,1,0:T(1,128)}), f32[128,1,2304]{2,1,0:T(1,128)}, u32[]{:S(2)}, u32[]{:S(2)}) async-start(f32[128,1,2304]{2,1,0:T(1,128)} %reshape.4455), calls=%async_computation.4 | async-start | bytes 2359296 | tf_op jit(solution)/shard_map/all_to_all | solution.py:84
  1477.1 25.0 %all-to-all-start.5 = ((f32[128,1,2304]{2,1,0:T(1,128)}), f32[128,1,2304]{2,1,0:T(1,128)}, u32[]{:S(2)}, u32[]{:S(2)}) async-start(f32[128,1,2304]{2,1,0:T(1,128)} %reshape.4457), calls=%async_computation.5 | async-start | bytes 2359296 | tf_op jit(solution)/shard_map/all_to_all | solution.py:84
  1543.2 199.0 %copy-start.4 = (f32[2,24,24,128]{3,2,1,0:T(8,128)}, f32[2,24,24,128]{3,2,1,0:T(8,128)S(1)}, u32[]{:S(2)}) copy-start(f32[2,24,24,128]{3,2,1,0:T(8,128)S(1)} %copy.2086) | copy-start | bytes 1769476
  1735.1 25.0 %all-to-all-start.6 = ((f32[128,1,2304]{2,1,0:T(1,128)}), f32[128,1,2304]{2,1,0:T(1,128)}, u32[]{:S(2)}, u32[]{:S(2)}) async-start(f32[128,1,2304]{2,1,0:T(1,128)} %reshape.4459), calls=%async_computation.6 | async-start | bytes 2359296 | tf_op jit(solution)/shard_map/all_to_all | solution.py:84
